TPU v7x, 32 devices: a whole 2x2x4 slice. The times are simulated.
32 devices in a mesh: section: 8 (over z, x), expert: 4 (over y, core).
Axes of the slice: x: 2, y: 2, z: 4, core: 2. Of those that a mesh axis runs over, the one named last changes fastest.
Arguments:
- tokens: bfloat16 [16, 32, 768], P(None, 'expert'), may hold values from -6 to 6
- route_ids: int32 [8, 16, 32, 2], P('section'), may hold values from 0 to 3, all different within a row; in each aligned block of 8 rows (0 to 7, 8 to 15, ..., all dimensions but the last counted through in order) at most 8 rows name the same one
- router: bfloat16 [8, 768, 4], P('section'), may hold values from -0.21875 to 0.21875
- norm_gain: float32 [8, 768], P('section'), may hold values from 0.1 to 1.9
- weight_in: bfloat16 [8, 4, 768, 3072], P('section', 'expert'), may hold values from -0.21875 to 0.21875
- weight_out: bfloat16 [8, 4, 3072, 768], P('section', 'expert'), may hold values from -0.109375 to 0.109375
Outputs:
- layer_states: bfloat16 [8, 16, 32, 768], P('section', None, 'expert')
Inputs may be any that keep to these rules, and one draw needn't show every extreme that they name: `route_ids`: each row names two different experts. In each aligned block of 8 rows (the tokens of one micro-batch on one index of the expert axis) no expert is named by more than 8 rows, and in some blocks one expert is named by exactly 8.
All inputs are finite; a program needn't handle non-finite values.
Results may differ from a plain program's by a relative error of at most 0.028.
Values may be sent and summed in bfloat16 or wider, within the bound.
No kernel may reach another device: no remote copies, remote signals or barrier semaphores. Data moves between devices by JAX's collectives and lax.ppermute only.
A program may use at most 64 MiB of HBM per device.

v0:
```python
import functools

import jax
import jax.numpy as jnp
from jax import lax
from jax.experimental import pallas as pl
from jax.experimental.pallas import tpu as pltpu
from jax.sharding import PartitionSpec as P


epsilon = 1e-06
STREAMS = 2
GROUPS = 2
LANES = 128
UNROLLED = 32


def expert_kernel(
    parts, mine_ref, other_ref, mask_ref, gain_ref, router_ref, in_ref, out_ref, behind_ref,
    send_ref, keep_ref, total_ref,
):
    half, features = mine_ref.shape
    block = min(half, 64)

    def group(g, carry):
        rows = pl.ds(pl.multiple_of(g * block, block), block)
        lower = pl.ds(pl.multiple_of(half + g * block, block), block)

        def normed_of(ref):
            stream = ref[rows, :].astype(jnp.float32)
            inverse = lax.rsqrt(jnp.mean(stream * stream, axis=-1, keepdims=True) + epsilon)
            return (stream * inverse * gain_ref[...]).astype(jnp.bfloat16)

        normed = jnp.concatenate([normed_of(mine_ref), normed_of(other_ref)], axis=0)
        logits = jnp.dot(normed, router_ref[...], preferred_element_type=jnp.float32)
        mask = jnp.concatenate([mask_ref[rows, :], mask_ref[lower, :]], axis=0)
        gate = jax.nn.sigmoid(logits) * mask
        tile = in_ref.shape[1] // parts

        def product(i):
            some = pl.ds(pl.multiple_of(i * tile, tile), tile)
            hidden = jnp.dot(normed, in_ref[:, some], preferred_element_type=jnp.float32)
            hidden = jnp.maximum(hidden, 0.0).astype(jnp.bfloat16)
            return jnp.dot(hidden, out_ref[some, :], preferred_element_type=jnp.float32)

        if parts == 1:
            total = product(0)
        else:
            total_ref[...] = jnp.zeros_like(total_ref)

            def add(i, none):
                total_ref[...] += product(i)
                return none

            lax.fori_loop(0, parts, add, 0)
            total = total_ref[...]
        for column in range(0, features, LANES):
            lanes = slice(column, column + LANES)
            gated = (total[:, lanes] * gate).astype(send_ref.dtype)
            send_ref[rows, lanes] = gated[:block]
            keep_ref[rows, lanes] = gated[block:]
        return carry

    if half == block:
        group(0, 0)
    else:
        lax.fori_loop(0, half // block, group, 0)


def load_kernel(in_ref, out_ref, in_local, out_local, sems):
    pieces = sems.shape[1]
    copies = []
    for n, (source, target) in enumerate(((in_ref, in_local), (out_ref, out_local))):
        size = source.shape[0] // pieces
        for i in range(pieces):
            part = pl.ds(i * size, size)
            copies.append(
                pltpu.make_async_copy(source.at[part, :], target.at[part, :], sems.at[n, i])
            )
    for copy in copies:
        copy.start()
    for copy in copies:
        copy.wait()


def load(weight_in, weight_out):
    local = pl.BlockSpec(memory_space=pltpu.VMEM)
    return pl.pallas_call(
        load_kernel,
        out_shape=tuple(jax.ShapeDtypeStruct(w.shape, w.dtype) for w in (weight_in, weight_out)),
        in_specs=[pl.BlockSpec(memory_space=pltpu.HBM)] * 2,
        out_specs=(local,) * 2,
        scratch_shapes=[pltpu.SemaphoreType.DMA((2, 4))],
        compiler_params=pltpu.CompilerParams(vmem_limit_bytes=43 * 2**20),
        cost_estimate=pl.CostEstimate(
            flops=2 * weight_in.size * 1024, bytes_accessed=8 * weight_in.size, transcendentals=0
        ),
    )(weight_in, weight_out)


def run_expert(parts, mine, other, mask, gain, router, weight_in, weight_out, behind):
    half, features = mine.shape
    hidden_total = weight_in.shape[1]
    local = pl.BlockSpec(memory_space=pltpu.VMEM)
    return pl.pallas_call(
        functools.partial(expert_kernel, parts),
        out_shape=(jax.ShapeDtypeStruct(mine.shape, jnp.bfloat16),) * 2,
        in_specs=[local] * 7 + [pl.BlockSpec(memory_space=pl.ANY)],
        out_specs=(local,) * 2,
        scratch_shapes=[pltpu.VMEM((2 * min(half, 64), features), jnp.float32)],
        compiler_params=pltpu.CompilerParams(vmem_limit_bytes=20 * 2**20),
        cost_estimate=pl.CostEstimate(
            flops=8 * half * features * hidden_total,
            bytes_accessed=4 * features * hidden_total,
            transcendentals=0,
        ),
    )(mine, other, mask, gain, router, weight_in, weight_out, behind)


def body(tokens, route_ids, router, norm_gain, weight_in, weight_out):
    sections, experts = lax.axis_size("section"), lax.axis_size("expert")
    section, member = lax.axis_index("section"), lax.axis_index("expert")
    chip, core = member // 2, member % 2
    chips = experts // 2
    micro_count, tok_rows, features = tokens.shape
    pieces = STREAMS * GROUPS
    part = micro_count // pieces
    rows = part * tok_rows
    gain = norm_gain.astype(jnp.float32)
    expert_in, expert_out = weight_in[0, 0], weight_out[0, 0]
    column = lax.dynamic_slice_in_dim(router[0], member, 1, axis=1)
    column = jnp.broadcast_to(column, (features, LANES))

    named = jnp.any(route_ids[0] == member, axis=-1)
    named = named.reshape(GROUPS, STREAMS, part, chips, 2, tok_rows).transpose(1, 0, 4, 3, 2, 5)
    named = jnp.where(core == 0, named[:, :, ::-1], named).astype(jnp.float32)
    masks = named.reshape(STREAMS, GROUPS, experts * rows, 1)
    masks = jnp.broadcast_to(masks, masks.shape[:3] + (LANES,))

    def place(s, e):
        return s * experts + e

    def across(value, other_of):
        pairs = [
            (place(s, e), place(*other_of(s, e))) for s in range(sections) for e in range(experts)
        ]
        return lax.ppermute(value, ("section", "expert"), pairs)

    def to_paired(value, odd, flip):
        def other_of(s, e):
            other = s - 1 if (s % 2 == 0) == odd else s + 1
            if 0 <= other < sections:
                return (other, e ^ flip)
            return (s, e ^ (flip or 1))

        return across(value, other_of)

    def swapped(value):
        return across(value, lambda s, e: (s, e ^ 1))

    def from_chips(value):
        return [across(value, lambda s, e, k=k: (s, e ^ (2 * k + 1))) for k in range(chips)]

    own_tokens = tokens.reshape(-1, features)
    first, later = from_chips(own_tokens[:rows]), from_chips(own_tokens[rows:])
    turns = sections + 2 * (GROUPS - 1)
    facts = {
        "at": [section == turn for turn in range(turns)],
        "index": [
            jnp.clip((turn - section) // 2, 0, GROUPS - 1).astype(jnp.int32)
            for turn in range(turns)
        ],
        "start": [(chip ^ k) * rows for k in range(chips)],
        "between": [[(chip ^ y) == k for k in range(chips)] for y in range(chips)],
        "lead": chip == 0,
        "even": section % 2 == 0,
    }
    facts, masks, column, expert_in, expert_out = lax.optimization_barrier(
        (facts, masks, column, expert_in, expert_out)
    )
    expert_in, expert_out = load(expert_in, expert_out)

    def by_chip(came, at):
        halves = []
        for y in range(chips):
            wanted = came[0]
            for k in range(1, chips):
                wanted = jnp.where(facts["between"][y][k], came[k], wanted)
            halves.append(wanted[at * rows : (at + 1) * rows])
        return jnp.concatenate(halves, axis=0)

    entering = [by_chip(first, 0)] + [by_chip(later, n) for n in range(pieces - 1)]

    def known(name, turn):
        if isinstance(turn, int):
            return facts[name][turn]
        if name == "at":
            return section == turn
        return jnp.clip((turn - section) // 2, 0, GROUPS - 1)

    def own_of(other, k=0):
        start = (facts["start"][k], jnp.zeros_like(facts["start"][k]))
        return lax.dynamic_slice(
            other, start, (rows, features), allow_negative_indices=False
        )

    arrived = [
        [entering[q]] + [jnp.zeros_like(entering[q])] * (chips - 1) for q in range(STREAMS)
    ]
    blank = jnp.zeros((rows, features), jnp.bfloat16)
    saved = [[blank] * GROUPS for _ in range(STREAMS)]
    final = [[blank] * GROUPS for _ in range(STREAMS)]

    def whole(values):
        return jnp.stack([values[q][i] for i in range(GROUPS) for q in range(STREAMS)])

    def one_turn(turn, odd, state, ending=False):
        arrived, saved, final, behind = state
        arrived = [list(x) for x in arrived]
        saved, final = [list(x) for x in saved], [list(x) for x in final]
        for q in range(STREAMS):
            late = STREAMS - 1 - q
            if behind is not None:
                before = odd if q > 0 else not odd
                arrived[late] = []
                for k in range(chips):
                    arrived[late].append(to_paired(behind, before, 2 * k + 1))
                arrived[q] = list(lax.optimization_barrier((behind, *arrived[q])))[1:]
            mine = sum(a.astype(jnp.float32) for a in arrived[q]).astype(jnp.bfloat16)
            if not odd:
                for i in range(1, GROUPS):
                    fresh = facts["at"][0]
                    if not isinstance(turn, int):
                        fresh = jnp.logical_and(fresh, turn == 2 * i)
                    elif turn != 2 * i:
                        continue
                    mine = jnp.where(fresh, entering[i * STREAMS + q], mine)
            other = swapped(mine)
            own = own_of(other)
            for i in range(GROUPS):
                if not isinstance(turn, int):
                    ended = turn == sections + 2 * i
                    final[q][i] = jnp.where(ended, own, final[q][i])
                elif turn == sections + 2 * i:
                    final[q][i] = own
                if not isinstance(turn, int) or 1 <= turn - 2 * i < sections:
                    here = known("at", turn - 2 * i)
                    saved[q][i] = jnp.where(here, own, saved[q][i])
            returned = None
            if ending and q == STREAMS - 1:
                passed = whole(saved).reshape(-1, features)
                from_even = to_paired(passed, False, 0)
                from_odd = to_paired(passed, True, 0)
                returned = jnp.where(facts["even"], from_even, from_odd)
            index = known("index", turn)
            nought = jnp.zeros_like(index)
            mask = lax.dynamic_slice(
                masks[q], (index, nought, nought), (1,) + masks.shape[2:],
                allow_negative_indices=False,
            )[0]
            send, keep = run_expert(
                2 if odd == (q > 0) else 1, mine, other, mask, gain, column, expert_in, expert_out,
                mine if behind is None else behind,
            )
            came = swapped(send)
            stream = jnp.where(facts["lead"], other, jnp.zeros_like(other)).astype(jnp.float32)
            partial = keep.astype(jnp.float32) + came.astype(jnp.float32) + stream
            behind = partial.astype(jnp.bfloat16)
            if ending:
                own = own_of(partial)
                for k in range(1, chips):
                    own = own + across(
                        own_of(behind, k), lambda s, e, k=k: (s, e ^ (2 * k))
                    ).astype(jnp.float32)
                final[q][GROUPS - 1] = own.astype(jnp.bfloat16)
                if q == 0:
                    behind = None
        if ending:
            return final, returned
        return arrived, saved, final, behind

    def two_turns(pair, state):
        return one_turn(2 * pair + 1, True, one_turn(2 * pair, False, state))

    state = two_turns(0, (arrived, saved, final, None))
    if sections * chips <= UNROLLED:
        for pair in range(1, turns // 2 - 1):
            state = two_turns(pair, state)
    else:
        state = lax.fori_loop(1, turns // 2 - 1, two_turns, state)
    state = one_turn(turns - 2, False, state)
    final, returned = one_turn(turns - 1, True, state, ending=True)

    states = jnp.where(facts["at"][sections - 1], whole(final).reshape(-1, features), returned)
    return states.reshape(1, micro_count, tok_rows, features)


def solution(mesh):
    placed = (
        P(None, "expert", None),
        P("section", None, None, None),
        P("section", None, None),
        P("section", None),
        P("section", "expert", None, None),
        P("section", "expert", None, None),
    )
    return jax.shard_map(
        body,
        mesh=mesh,
        in_specs=placed,
        out_specs=P("section", None, "expert", None),
        check_vma=False,
    )
```

profile of v0, /device:TPU:8, one launch (start us, length us, event | category | flops | bytes accessed | tf_op | source)
XLA Modules:
  0.0 225.6 jit_solution(2252426137627002311)
XLA Ops:
  5.4 3.8 %shard_map.64 = (bf16[768,3072]{1,0:T(8,128)(2,1)S(1)}, bf16[3072,768]{1,0:T(8,128)(2,1)S(1)}) custom-call(bf16[768,3072]{1,0:T(8,128)(2,1)} %bitcast.72, bf16[3072,768]{1,0:T(8,128)(2,1)} %bitcast.73), custom_call_target="tpu_custom_call" | custom-call | flops 4831838208 | bytes 18874368 | tf_op jit(solution)/shard_map/pallas_call | solution.py:88
  22.2 3.0 %collective-permute-done.9 = bf16[64,768]{1,0:T(8,128)(2,1)S(1)} collective-permute-done((bf16[64,768]{1,0:T(8,128)(2,1)S(1)}, bf16[64,768]{1,0:T(8,128)(2,1)S(1)}, u32[]{:S(2)}, u32[]{:S(2)}) %collective-permute-start.9) | collective-permute-done | bytes 98336 | tf_op jit(solution)/shard_map/ppermute | solution.py:147
  30.6 2.7 %collective-permute-done.12 = bf16[64,768]{1,0:T(8,128)(2,1)S(1)} collective-permute-done((bf16[64,768]{1,0:T(8,128)(2,1)S(1)}, bf16[64,768]{1,0:T(8,128)(2,1)S(1)}, u32[]{:S(2)}, u32[]{:S(2)}) %collective-permute-start.12) | collective-permute-done | bytes 98336 | tf_op jit(solution)/shard_map/ppermute | solution.py:147
  33.3 2.3 %collective-permute-done.13 = bf16[64,768]{1,0:T(8,128)(2,1)S(1)} collective-permute-done((bf16[64,768]{1,0:T(8,128)(2,1)S(1)}, bf16[64,768]{1,0:T(8,128)(2,1)S(1)}, u32[]{:S(2)}, u32[]{:S(2)}) %collective-permute-start.13) | collective-permute-done | bytes 98336 | tf_op jit(solution)/shard_map/ppermute | solution.py:147
  40.5 2.3 %collective-permute-start.17 = (bf16[64,768]{1,0:T(8,128)(2,1)S(1)}, bf16[64,768]{1,0:T(8,128)(2,1)S(1)}, u32[]{:S(2)}, u32[]{:S(2)}) collective-permute-start(bf16[64,768]{1,0:T(8,128)(2,1)S(1)} %add_convert_fusion.32.behind_ref), channel_id=1, source_target_pairs={{0,3},{1,2},{2,1},{3,0},{4,11},{5,10},{6,9},{7,8},{8,7},{9,6},{10,... | collective-permute-start | bytes 294920 | tf_op jit(solution)/shard_map/ppermute | solution.py:147
  45.0 2.8 %collective-permute-done.17 = bf16[64,768]{1,0:T(8,128)(2,1)S(1)} collective-permute-done((bf16[64,768]{1,0:T(8,128)(2,1)S(1)}, bf16[64,768]{1,0:T(8,128)(2,1)S(1)}, u32[]{:S(2)}, u32[]{:S(2)}) %collective-permute-start.17) | collective-permute-done | bytes 98336 | tf_op jit(solution)/shard_map/ppermute | solution.py:147
  54.8 2.6 %collective-permute-done.20 = bf16[64,768]{1,0:T(8,128)(2,1)S(1)} collective-permute-done((bf16[64,768]{1,0:T(8,128)(2,1)S(1)}, bf16[64,768]{1,0:T(8,128)(2,1)S(1)}, u32[]{:S(2)}, u32[]{:S(2)}) %collective-permute-start.20) | collective-permute-done | bytes 98336 | tf_op jit(solution)/shard_map/ppermute | solution.py:147
  57.4 2.6 %collective-permute-done.21 = bf16[64,768]{1,0:T(8,128)(2,1)S(1)} collective-permute-done((bf16[64,768]{1,0:T(8,128)(2,1)S(1)}, bf16[64,768]{1,0:T(8,128)(2,1)S(1)}, u32[]{:S(2)}, u32[]{:S(2)}) %collective-permute-start.21) | collective-permute-done | bytes 98336 | tf_op jit(solution)/shard_map/ppermute | solution.py:147
  65.4 2.3 %collective-permute-done.24 = bf16[64,768]{1,0:T(8,128)(2,1)S(1)} collective-permute-done((bf16[64,768]{1,0:T(8,128)(2,1)S(1)}, bf16[64,768]{1,0:T(8,128)(2,1)S(1)}, u32[]{:S(2)}, u32[]{:S(2)}) %collective-permute-start.24) | collective-permute-done | bytes 98336 | tf_op jit(solution)/shard_map/ppermute | solution.py:147
  67.7 2.8 %collective-permute-done.25 = bf16[64,768]{1,0:T(8,128)(2,1)S(1)} collective-permute-done((bf16[64,768]{1,0:T(8,128)(2,1)S(1)}, bf16[64,768]{1,0:T(8,128)(2,1)S(1)}, u32[]{:S(2)}, u32[]{:S(2)}) %collective-permute-start.25) | collective-permute-done | bytes 98336 | tf_op jit(solution)/shard_map/ppermute | solution.py:147
  76.1 2.3 collective-permute-done.28
  78.3 2.7 %collective-permute-done.29 = bf16[64,768]{1,0:T(8,128)(2,1)S(1)} collective-permute-done((bf16[64,768]{1,0:T(8,128)(2,1)S(1)}, bf16[64,768]{1,0:T(8,128)(2,1)S(1)}, u32[]{:S(2)}, u32[]{:S(2)}) %collective-permute-start.29) | collective-permute-done | bytes 98336 | tf_op jit(solution)/shard_map/ppermute | solution.py:147
  82.4 2.4 %shard_map.72 = (bf16[64,768]{1,0:T(8,128)(2,1)S(1)}, bf16[64,768]{1,0:T(8,128)(2,1)S(1)}) custom-call(bf16[64,768]{1,0:T(8,128)(2,1)S(1)} %add_convert_fusion.23.mine_ref, bf16[64,768]{1,0:T(8,128)(2,1)S(1)} %collective-permute-done.30.other_ref, f32[128,128]{1,0:T(8,128)S(1)} %get-tuple-element.247.mask_ref, f32[1,768]{1,0:T(1,128)S(1)} %copy-done.1, ...), custom_call_target="tpu_custom_call" | custom-call | flops 1207959552 | bytes 9437184 | tf_op jit(solution)/shard_map/pallas_call | solution.py:105
  88.2 2.5 %collective-permute-done.32 = bf16[64,768]{1,0:T(8,128)(2,1)S(1)} collective-permute-done((bf16[64,768]{1,0:T(8,128)(2,1)S(1)}, bf16[64,768]{1,0:T(8,128)(2,1)S(1)}, u32[]{:S(2)}, u32[]{:S(2)}) %collective-permute-start.32) | collective-permute-done | bytes 98336 | tf_op jit(solution)/shard_map/ppermute | solution.py:147
  90.7 2.6 %collective-permute-done.33 = bf16[64,768]{1,0:T(8,128)(2,1)S(1)} collective-permute-done((bf16[64,768]{1,0:T(8,128)(2,1)S(1)}, bf16[64,768]{1,0:T(8,128)(2,1)S(1)}, u32[]{:S(2)}, u32[]{:S(2)}) %collective-permute-start.33) | collective-permute-done | bytes 98336 | tf_op jit(solution)/shard_map/ppermute | solution.py:147
  100.3 2.3 %collective-permute-done.36 = bf16[64,768]{1,0:T(8,128)(2,1)S(1)} collective-permute-done((bf16[64,768]{1,0:T(8,128)(2,1)S(1)}, bf16[64,768]{1,0:T(8,128)(2,1)S(1)}, u32[]{:S(2)}, u32[]{:S(2)}) %collective-permute-start.36) | collective-permute-done | bytes 98336 | tf_op jit(solution)/shard_map/ppermute | solution.py:147
  102.6 2.9 %collective-permute-done.37 = bf16[64,768]{1,0:T(8,128)(2,1)S(1)} collective-permute-done((bf16[64,768]{1,0:T(8,128)(2,1)S(1)}, bf16[64,768]{1,0:T(8,128)(2,1)S(1)}, u32[]{:S(2)}, u32[]{:S(2)}) %collective-permute-start.37) | collective-permute-done | bytes 98336 | tf_op jit(solution)/shard_map/ppermute | solution.py:147
  110.8 2.5 %collective-permute-done.40 = bf16[64,768]{1,0:T(8,128)(2,1)S(1)} collective-permute-done((bf16[64,768]{1,0:T(8,128)(2,1)S(1)}, bf16[64,768]{1,0:T(8,128)(2,1)S(1)}, u32[]{:S(2)}, u32[]{:S(2)}) %collective-permute-start.40) | collective-permute-done | bytes 98336 | tf_op jit(solution)/shard_map/ppermute | solution.py:147
  113.2 2.6 %collective-permute-done.41 = bf16[64,768]{1,0:T(8,128)(2,1)S(1)} collective-permute-done((bf16[64,768]{1,0:T(8,128)(2,1)S(1)}, bf16[64,768]{1,0:T(8,128)(2,1)S(1)}, u32[]{:S(2)}, u32[]{:S(2)}) %collective-permute-start.41) | collective-permute-done | bytes 98336 | tf_op jit(solution)/shard_map/ppermute | solution.py:147
  123.8 2.8 %collective-permute-done.45 = bf16[64,768]{1,0:T(8,128)(2,1)S(1)} collective-permute-done((bf16[64,768]{1,0:T(8,128)(2,1)S(1)}, bf16[64,768]{1,0:T(8,128)(2,1)S(1)}, u32[]{:S(2)}, u32[]{:S(2)}) %collective-permute-start.45) | collective-permute-done | bytes 98336 | tf_op jit(solution)/shard_map/ppermute | solution.py:147
  133.3 2.7 %collective-permute-done.48 = bf16[64,768]{1,0:T(8,128)(2,1)S(1)} collective-permute-done((bf16[64,768]{1,0:T(8,128)(2,1)S(1)}, bf16[64,768]{1,0:T(8,128)(2,1)S(1)}, u32[]{:S(2)}, u32[]{:S(2)}) %collective-permute-start.48) | collective-permute-done | bytes 98336 | tf_op jit(solution)/shard_map/ppermute | solution.py:147
  136.0 2.4 %collective-permute-done.49 = bf16[64,768]{1,0:T(8,128)(2,1)S(1)} collective-permute-done((bf16[64,768]{1,0:T(8,128)(2,1)S(1)}, bf16[64,768]{1,0:T(8,128)(2,1)S(1)}, u32[]{:S(2)}, u32[]{:S(2)}) %collective-permute-start.49) | collective-permute-done | bytes 98336 | tf_op jit(solution)/shard_map/ppermute | solution.py:147
  139.8 2.4 %shard_map.77 = (bf16[64,768]{1,0:T(8,128)(2,1)S(1)}, bf16[64,768]{1,0:T(8,128)(2,1)S(1)}) custom-call(bf16[64,768]{1,0:T(8,128)(2,1)S(1)} %add_convert_fusion.13.mine_ref, bf16[64,768]{1,0:T(8,128)(2,1)S(1)} %collective-permute-done.50.other_ref, f32[128,128]{1,0:T(8,128)S(1)} %get-tuple-element.234.mask_ref, f32[1,768]{1,0:T(1,128)S(1)} %copy-done.1, ...), custom_call_target="tpu_custom_call" | custom-call | flops 1207959552 | bytes 9437184 | tf_op jit(solution)/shard_map/pallas_call | solution.py:105
  147.9 3.1 %collective-permute-done.53 = bf16[64,768]{1,0:T(8,128)(2,1)S(1)} collective-permute-done((bf16[64,768]{1,0:T(8,128)(2,1)S(1)}, bf16[64,768]{1,0:T(8,128)(2,1)S(1)}, u32[]{:S(2)}, u32[]{:S(2)}) %collective-permute-start.53) | collective-permute-done | bytes 98336 | tf_op jit(solution)/shard_map/ppermute | solution.py:147
  156.3 2.5 %collective-permute-done.56 = bf16[64,768]{1,0:T(8,128)(2,1)S(1)} collective-permute-done((bf16[64,768]{1,0:T(8,128)(2,1)S(1)}, bf16[64,768]{1,0:T(8,128)(2,1)S(1)}, u32[]{:S(2)}, u32[]{:S(2)}) %collective-permute-start.56) | collective-permute-done | bytes 98336 | tf_op jit(solution)/shard_map/ppermute | solution.py:147
  158.8 2.5 %collective-permute-done.57 = bf16[64,768]{1,0:T(8,128)(2,1)S(1)} collective-permute-done((bf16[64,768]{1,0:T(8,128)(2,1)S(1)}, bf16[64,768]{1,0:T(8,128)(2,1)S(1)}, u32[]{:S(2)}, u32[]{:S(2)}) %collective-permute-start.57) | collective-permute-done | bytes 98336 | tf_op jit(solution)/shard_map/ppermute | solution.py:147
  169.3 2.8 %collective-permute-done.61 = bf16[64,768]{1,0:T(8,128)(2,1)S(1)} collective-permute-done((bf16[64,768]{1,0:T(8,128)(2,1)S(1)}, bf16[64,768]{1,0:T(8,128)(2,1)S(1)}, u32[]{:S(2)}, u32[]{:S(2)}) %collective-permute-start.61) | collective-permute-done | bytes 98336 | tf_op jit(solution)/shard_map/ppermute | solution.py:147
  178.8 2.8 %collective-permute-done.64 = bf16[64,768]{1,0:T(8,128)(2,1)S(1)} collective-permute-done((bf16[64,768]{1,0:T(8,128)(2,1)S(1)}, bf16[64,768]{1,0:T(8,128)(2,1)S(1)}, u32[]{:S(2)}, u32[]{:S(2)}) %collective-permute-start.64) | collective-permute-done | bytes 98336 | tf_op jit(solution)/shard_map/ppermute | solution.py:147
  181.6 2.3 %collective-permute-done.65 = bf16[64,768]{1,0:T(8,128)(2,1)S(1)} collective-permute-done((bf16[64,768]{1,0:T(8,128)(2,1)S(1)}, bf16[64,768]{1,0:T(8,128)(2,1)S(1)}, u32[]{:S(2)}, u32[]{:S(2)}) %collective-permute-start.65) | collective-permute-done | bytes 98336 | tf_op jit(solution)/shard_map/ppermute | solution.py:147
  193.2 3.1 %collective-permute-done.69 = bf16[64,768]{1,0:T(8,128)(2,1)S(1)} collective-permute-done((bf16[64,768]{1,0:T(8,128)(2,1)S(1)}, bf16[64,768]{1,0:T(8,128)(2,1)S(1)}, u32[]{:S(2)}, u32[]{:S(2)}) %collective-permute-start.69) | collective-permute-done | bytes 98336 | tf_op jit(solution)/shard_map/ppermute | solution.py:147
  204.1 2.6 %collective-permute-done.73 = bf16[64,768]{1,0:T(8,128)(2,1)S(1)} collective-permute-done((bf16[64,768]{1,0:T(8,128)(2,1)S(1)}, bf16[64,768]{1,0:T(8,128)(2,1)S(1)}, u32[]{:S(2)}, u32[]{:S(2)}) %collective-permute-start.73) | collective-permute-done | bytes 98336 | tf_op jit(solution)/shard_map/ppermute | solution.py:147
  208.6 2.3 %collective-permute-done.78 = bf16[64,768]{1,0:T(8,128)(2,1)S(1)} collective-permute-done((bf16[64,768]{1,0:T(8,128)(2,1)S(1)}, bf16[64,768]{1,0:T(8,128)(2,1)S(1)}, u32[]{:S(2)}, u32[]{:S(2)}) %collective-permute-start.78) | collective-permute-done | bytes 98336 | tf_op jit(solution)/shard_map/ppermute | solution.py:147
  (228 shorter events, 141.1 us)
Async XLA Ops:
  0.8 8.4 %collective-permute-start.2 = (bf16[32,768]{1,0:T(8,128)(2,1)S(1)}, bf16[32,768]{1,0:T(8,128)(2,1)S(1)}, u32[]{:S(2)}, u32[]{:S(2)}) collective-permute-start(bf16[32,768]{1,0:T(8,128)(2,1)S(1)} %slice_bitcast_fusion.1), channel_id=1, source_target_pairs={{0,3},{1,2},{2,1},{3,0},{4,7},{5,6},{6,5},{7,4},{8,11},{9,10},{10,... | collective-permute-start | bytes 147464 | tf_op jit(solution)/shard_map/ppermute | solution.py:147
  1.8 7.5 %collective-permute-start.3 = (bf16[32,768]{1,0:T(8,128)(2,1)S(1)}, bf16[32,768]{1,0:T(8,128)(2,1)S(1)}, u32[]{:S(2)}, u32[]{:S(2)}) collective-permute-start(bf16[32,768]{1,0:T(8,128)(2,1)S(1)} %slice_bitcast_fusion.1), channel_id=1, source_target_pairs={{0,1},{1,0},{2,3},{3,2},{4,5},{5,4},{6,7},{7,6},{8,9},{9,8},{10,11... | collective-permute-start | bytes 147464 | tf_op jit(solution)/shard_map/ppermute | solution.py:147
  3.4 9.7 %collective-permute-start = (bf16[96,768]{1,0:T(8,128)(2,1)S(1)}, bf16[96,768]{1,0:T(8,128)(2,1)S(1)}, u32[]{:S(2)}, u32[]{:S(2)}) collective-permute-start(bf16[96,768]{1,0:T(8,128)(2,1)S(1)} %slice_bitcast_fusion), channel_id=1, source_target_pairs={{0,3},{1,2},{2,1},{3,0},{4,7},{5,6},{6,5},{7,4},{8,11},{9,10},{10,... | collective-permute-start | bytes 442376 | tf_op jit(solution)/shard_map/ppermute | solution.py:147
  3.6 9.5 %collective-permute-start.1 = (bf16[96,768]{1,0:T(8,128)(2,1)S(1)}, bf16[96,768]{1,0:T(8,128)(2,1)S(1)}, u32[]{:S(2)}, u32[]{:S(2)}) collective-permute-start(bf16[96,768]{1,0:T(8,128)(2,1)S(1)} %slice_bitcast_fusion), channel_id=1, source_target_pairs={{0,1},{1,0},{2,3},{3,2},{4,5},{5,4},{6,7},{7,6},{8,9},{9,8},{10,11... | collective-permute-start | bytes 442376 | tf_op jit(solution)/shard_map/ppermute | solution.py:147
  19.0 6.2 %collective-permute-start.9 = (bf16[64,768]{1,0:T(8,128)(2,1)S(1)}, bf16[64,768]{1,0:T(8,128)(2,1)S(1)}, u32[]{:S(2)}, u32[]{:S(2)}) collective-permute-start(bf16[64,768]{1,0:T(8,128)(2,1)S(1)} %add_convert_fusion.36.behind_ref), channel_id=1, source_target_pairs={{0,7},{1,6},{2,5},{3,4},{4,3},{5,2},{6,1},{7,0},{8,15},{9,14},{10,... | collective-permute-start | bytes 294920 | tf_op jit(solution)/shard_map/ppermute | solution.py:147
  29.9 5.8 %collective-permute-start.13 = (bf16[64,768]{1,0:T(8,128)(2,1)S(1)}, bf16[64,768]{1,0:T(8,128)(2,1)S(1)}, u32[]{:S(2)}, u32[]{:S(2)}) collective-permute-start(bf16[64,768]{1,0:T(8,128)(2,1)S(1)} %add_convert_fusion.34.behind_ref), channel_id=1, source_target_pairs={{0,7},{1,6},{2,5},{3,4},{4,3},{5,2},{6,1},{7,0},{8,15},{9,14},{10,... | collective-permute-start | bytes 294920 | tf_op jit(solution)/shard_map/ppermute | solution.py:147
  40.5 7.2 %collective-permute-start.17 = (bf16[64,768]{1,0:T(8,128)(2,1)S(1)}, bf16[64,768]{1,0:T(8,128)(2,1)S(1)}, u32[]{:S(2)}, u32[]{:S(2)}) collective-permute-start(bf16[64,768]{1,0:T(8,128)(2,1)S(1)} %add_convert_fusion.32.behind_ref), channel_id=1, source_target_pairs={{0,3},{1,2},{2,1},{3,0},{4,11},{5,10},{6,9},{7,8},{8,7},{9,6},{10,... | collective-permute-start | bytes 294920 | tf_op jit(solution)/shard_map/ppermute | solution.py:147
  51.7 5.6 %collective-permute-start.20 = (bf16[64,768]{1,0:T(8,128)(2,1)S(1)}, bf16[64,768]{1,0:T(8,128)(2,1)S(1)}, u32[]{:S(2)}, u32[]{:S(2)}) collective-permute-start(bf16[64,768]{1,0:T(8,128)(2,1)S(1)} %add_convert_fusion.30.behind_ref), channel_id=1, source_target_pairs={{0,1},{1,0},{2,3},{3,2},{4,9},{5,8},{6,11},{7,10},{8,5},{9,4},{10,... | collective-permute-start | bytes 294920 | tf_op jit(solution)/shard_map/ppermute | solution.py:147
  53.0 6.9 %collective-permute-start.21 = (bf16[64,768]{1,0:T(8,128)(2,1)S(1)}, bf16[64,768]{1,0:T(8,128)(2,1)S(1)}, u32[]{:S(2)}, u32[]{:S(2)}) collective-permute-start(bf16[64,768]{1,0:T(8,128)(2,1)S(1)} %add_convert_fusion.30.behind_ref), channel_id=1, source_target_pairs={{0,3},{1,2},{2,1},{3,0},{4,11},{5,10},{6,9},{7,8},{8,7},{9,6},{10,... | collective-permute-start | bytes 294920 | tf_op jit(solution)/shard_map/ppermute | solution.py:147
  64.5 6.0 %collective-permute-start.25 = (bf16[64,768]{1,0:T(8,128)(2,1)S(1)}, bf16[64,768]{1,0:T(8,128)(2,1)S(1)}, u32[]{:S(2)}, u32[]{:S(2)}) collective-permute-start(bf16[64,768]{1,0:T(8,128)(2,1)S(1)} %add_convert_fusion.28.behind_ref), channel_id=1, source_target_pairs={{0,7},{1,6},{2,5},{3,4},{4,3},{5,2},{6,1},{7,0},{8,15},{9,14},{10,... | collective-permute-start | bytes 294920 | tf_op jit(solution)/shard_map/ppermute | solution.py:147
  75.1 6.0 %collective-permute-start.29 = (bf16[64,768]{1,0:T(8,128)(2,1)S(1)}, bf16[64,768]{1,0:T(8,128)(2,1)S(1)}, u32[]{:S(2)}, u32[]{:S(2)}) collective-permute-start(bf16[64,768]{1,0:T(8,128)(2,1)S(1)} %add_convert_fusion.26.behind_ref), channel_id=1, source_target_pairs={{0,7},{1,6},{2,5},{3,4},{4,3},{5,2},{6,1},{7,0},{8,15},{9,14},{10,... | collective-permute-start | bytes 294920 | tf_op jit(solution)/shard_map/ppermute | solution.py:147
  85.1 5.5 %collective-permute-start.32 = (bf16[64,768]{1,0:T(8,128)(2,1)S(1)}, bf16[64,768]{1,0:T(8,128)(2,1)S(1)}, u32[]{:S(2)}, u32[]{:S(2)}) collective-permute-start(bf16[64,768]{1,0:T(8,128)(2,1)S(1)} %add_convert_fusion.24.behind_ref), channel_id=1, source_target_pairs={{0,1},{1,0},{2,3},{3,2},{4,9},{5,8},{6,11},{7,10},{8,5},{9,4},{10,... | collective-permute-start | bytes 294920 | tf_op jit(solution)/shard_map/ppermute | solution.py:147
  86.2 7.1 %collective-permute-start.33 = (bf16[64,768]{1,0:T(8,128)(2,1)S(1)}, bf16[64,768]{1,0:T(8,128)(2,1)S(1)}, u32[]{:S(2)}, u32[]{:S(2)}) collective-permute-start(bf16[64,768]{1,0:T(8,128)(2,1)S(1)} %add_convert_fusion.24.behind_ref), channel_id=1, source_target_pairs={{0,3},{1,2},{2,1},{3,0},{4,11},{5,10},{6,9},{7,8},{8,7},{9,6},{10,... | collective-permute-start | bytes 294920 | tf_op jit(solution)/shard_map/ppermute | solution.py:147
  97.1 5.5 %collective-permute-start.36 = (bf16[64,768]{1,0:T(8,128)(2,1)S(1)}, bf16[64,768]{1,0:T(8,128)(2,1)S(1)}, u32[]{:S(2)}, u32[]{:S(2)}) collective-permute-start(bf16[64,768]{1,0:T(8,128)(2,1)S(1)} %add_convert_fusion.22.behind_ref), channel_id=1, source_target_pairs={{0,1},{1,0},{2,3},{3,2},{4,9},{5,8},{6,11},{7,10},{8,5},{9,4},{10,... | collective-permute-start | bytes 294920 | tf_op jit(solution)/shard_map/ppermute | solution.py:147
  98.6 6.9 %collective-permute-start.37 = (bf16[64,768]{1,0:T(8,128)(2,1)S(1)}, bf16[64,768]{1,0:T(8,128)(2,1)S(1)}, u32[]{:S(2)}, u32[]{:S(2)}) collective-permute-start(bf16[64,768]{1,0:T(8,128)(2,1)S(1)} %add_convert_fusion.22.behind_ref), channel_id=1, source_target_pairs={{0,3},{1,2},{2,1},{3,0},{4,11},{5,10},{6,9},{7,8},{8,7},{9,6},{10,... | collective-permute-start | bytes 294920 | tf_op jit(solution)/shard_map/ppermute | solution.py:147
  109.8 6.0 %collective-permute-start.41 = (bf16[64,768]{1,0:T(8,128)(2,1)S(1)}, bf16[64,768]{1,0:T(8,128)(2,1)S(1)}, u32[]{:S(2)}, u32[]{:S(2)}) collective-permute-start(bf16[64,768]{1,0:T(8,128)(2,1)S(1)} %add_convert_fusion.20.behind_ref), channel_id=1, source_target_pairs={{0,7},{1,6},{2,5},{3,4},{4,3},{5,2},{6,1},{7,0},{8,15},{9,14},{10,... | collective-permute-start | bytes 294920 | tf_op jit(solution)/shard_map/ppermute | solution.py:147
  120.6 6.0 %collective-permute-start.45 = (bf16[64,768]{1,0:T(8,128)(2,1)S(1)}, bf16[64,768]{1,0:T(8,128)(2,1)S(1)}, u32[]{:S(2)}, u32[]{:S(2)}) collective-permute-start(bf16[64,768]{1,0:T(8,128)(2,1)S(1)} %add_convert_fusion.18.behind_ref), channel_id=1, source_target_pairs={{0,7},{1,6},{2,5},{3,4},{4,3},{5,2},{6,1},{7,0},{8,15},{9,14},{10,... | collective-permute-start | bytes 294920 | tf_op jit(solution)/shard_map/ppermute | solution.py:147
  130.5 5.5 %collective-permute-start.48 = (bf16[64,768]{1,0:T(8,128)(2,1)S(1)}, bf16[64,768]{1,0:T(8,128)(2,1)S(1)}, u32[]{:S(2)}, u32[]{:S(2)}) collective-permute-start(bf16[64,768]{1,0:T(8,128)(2,1)S(1)} %add_convert_fusion.16.behind_ref), channel_id=1, source_target_pairs={{0,1},{1,0},{2,3},{3,2},{4,9},{5,8},{6,11},{7,10},{8,5},{9,4},{10,... | collective-permute-start | bytes 294920 | tf_op jit(solution)/shard_map/ppermute | solution.py:147
  131.3 7.0 %collective-permute-start.49 = (bf16[64,768]{1,0:T(8,128)(2,1)S(1)}, bf16[64,768]{1,0:T(8,128)(2,1)S(1)}, u32[]{:S(2)}, u32[]{:S(2)}) collective-permute-start(bf16[64,768]{1,0:T(8,128)(2,1)S(1)} %add_convert_fusion.16.behind_ref), channel_id=1, source_target_pairs={{0,3},{1,2},{2,1},{3,0},{4,11},{5,10},{6,9},{7,8},{8,7},{9,6},{10,... | collective-permute-start | bytes 294920 | tf_op jit(solution)/shard_map/ppermute | solution.py:147
  142.4 5.5 %collective-permute-start.52 = (bf16[64,768]{1,0:T(8,128)(2,1)S(1)}, bf16[64,768]{1,0:T(8,128)(2,1)S(1)}, u32[]{:S(2)}, u32[]{:S(2)}) collective-permute-start(bf16[64,768]{1,0:T(8,128)(2,1)S(1)} %add_convert_fusion.14.behind_ref), channel_id=1, source_target_pairs={{0,1},{1,0},{2,3},{3,2},{4,9},{5,8},{6,11},{7,10},{8,5},{9,4},{10,... | collective-permute-start | bytes 294920 | tf_op jit(solution)/shard_map/ppermute | solution.py:147
  144.1 6.9 %collective-permute-start.53 = (bf16[64,768]{1,0:T(8,128)(2,1)S(1)}, bf16[64,768]{1,0:T(8,128)(2,1)S(1)}, u32[]{:S(2)}, u32[]{:S(2)}) collective-permute-start(bf16[64,768]{1,0:T(8,128)(2,1)S(1)} %add_convert_fusion.14.behind_ref), channel_id=1, source_target_pairs={{0,3},{1,2},{2,1},{3,0},{4,11},{5,10},{6,9},{7,8},{8,7},{9,6},{10,... | collective-permute-start | bytes 294920 | tf_op jit(solution)/shard_map/ppermute | solution.py:147
  155.2 6.2 %collective-permute-start.57 = (bf16[64,768]{1,0:T(8,128)(2,1)S(1)}, bf16[64,768]{1,0:T(8,128)(2,1)S(1)}, u32[]{:S(2)}, u32[]{:S(2)}) collective-permute-start(bf16[64,768]{1,0:T(8,128)(2,1)S(1)} %add_convert_fusion.12.behind_ref), channel_id=1, source_target_pairs={{0,7},{1,6},{2,5},{3,4},{4,3},{5,2},{6,1},{7,0},{8,15},{9,14},{10,... | collective-permute-start | bytes 294920 | tf_op jit(solution)/shard_map/ppermute | solution.py:147
  166.1 6.0 %collective-permute-start.61 = (bf16[64,768]{1,0:T(8,128)(2,1)S(1)}, bf16[64,768]{1,0:T(8,128)(2,1)S(1)}, u32[]{:S(2)}, u32[]{:S(2)}) collective-permute-start(bf16[64,768]{1,0:T(8,128)(2,1)S(1)} %add_convert_fusion.10.behind_ref), channel_id=1, source_target_pairs={{0,7},{1,6},{2,5},{3,4},{4,3},{5,2},{6,1},{7,0},{8,15},{9,14},{10,... | collective-permute-start | bytes 294920 | tf_op jit(solution)/shard_map/ppermute | solution.py:147
  176.0 5.6 %collective-permute-start.64 = (bf16[64,768]{1,0:T(8,128)(2,1)S(1)}, bf16[64,768]{1,0:T(8,128)(2,1)S(1)}, u32[]{:S(2)}, u32[]{:S(2)}) collective-permute-start(bf16[64,768]{1,0:T(8,128)(2,1)S(1)} %add_convert_fusion.8.behind_ref), channel_id=1, source_target_pairs={{0,1},{1,0},{2,3},{3,2},{4,9},{5,8},{6,11},{7,10},{8,5},{9,4},{10,... | collective-permute-start | bytes 294920 | tf_op jit(solution)/shard_map/ppermute | solution.py:147
  176.7 7.2 %collective-permute-start.65 = (bf16[64,768]{1,0:T(8,128)(2,1)S(1)}, bf16[64,768]{1,0:T(8,128)(2,1)S(1)}, u32[]{:S(2)}, u32[]{:S(2)}) collective-permute-start(bf16[64,768]{1,0:T(8,128)(2,1)S(1)} %add_convert_fusion.8.behind_ref), channel_id=1, source_target_pairs={{0,3},{1,2},{2,1},{3,0},{4,11},{5,10},{6,9},{7,8},{8,7},{9,6},{10,... | collective-permute-start | bytes 294920 | tf_op jit(solution)/shard_map/ppermute | solution.py:147
  187.7 5.5 %collective-permute-start.68 = (bf16[64,768]{1,0:T(8,128)(2,1)S(1)}, bf16[64,768]{1,0:T(8,128)(2,1)S(1)}, u32[]{:S(2)}, u32[]{:S(2)}) collective-permute-start(bf16[64,768]{1,0:T(8,128)(2,1)S(1)} %add_convert_fusion.6.behind_ref), channel_id=1, source_target_pairs={{0,1},{1,0},{2,3},{3,2},{4,9},{5,8},{6,11},{7,10},{8,5},{9,4},{10,... | collective-permute-start | bytes 294920 | tf_op jit(solution)/shard_map/ppermute | solution.py:147
  189.4 6.9 %collective-permute-start.69 = (bf16[64,768]{1,0:T(8,128)(2,1)S(1)}, bf16[64,768]{1,0:T(8,128)(2,1)S(1)}, u32[]{:S(2)}, u32[]{:S(2)}) collective-permute-start(bf16[64,768]{1,0:T(8,128)(2,1)S(1)} %add_convert_fusion.6.behind_ref), channel_id=1, source_target_pairs={{0,3},{1,2},{2,1},{3,0},{4,11},{5,10},{6,9},{7,8},{8,7},{9,6},{10,... | collective-permute-start | bytes 294920 | tf_op jit(solution)/shard_map/ppermute | solution.py:147
  200.5 6.2 %collective-permute-start.73 = (bf16[64,768]{1,0:T(8,128)(2,1)S(1)}, bf16[64,768]{1,0:T(8,128)(2,1)S(1)}, u32[]{:S(2)}, u32[]{:S(2)}) collective-permute-start(bf16[64,768]{1,0:T(8,128)(2,1)S(1)} %add_convert_fusion.4.behind_ref), channel_id=1, source_target_pairs={{0,7},{1,6},{2,5},{3,4},{4,3},{5,2},{6,1},{7,0},{8,15},{9,14},{10,... | collective-permute-start | bytes 294920 | tf_op jit(solution)/shard_map/ppermute | solution.py:147
  201.6 7.0 %collective-permute-start.77 = (bf16[64,768]{1,0:T(8,128)(2,1)S(1)}, bf16[64,768]{1,0:T(8,128)(2,1)S(1)}, u32[]{:S(2)}, u32[]{:S(2)}) collective-permute-start(bf16[64,768]{1,0:T(8,128)(2,1)S(1)} %add_convert_fusion.2.behind_ref), channel_id=1, source_target_pairs={{0,5},{1,4},{2,7},{3,6},{4,1},{5,0},{6,3},{7,2},{8,13},{9,12},{10,... | collective-permute-start | bytes 294920 | tf_op jit(solution)/shard_map/ppermute | solution.py:147
  203.4 7.5 %collective-permute-start.78 = (bf16[64,768]{1,0:T(8,128)(2,1)S(1)}, bf16[64,768]{1,0:T(8,128)(2,1)S(1)}, u32[]{:S(2)}, u32[]{:S(2)}) collective-permute-start(bf16[64,768]{1,0:T(8,128)(2,1)S(1)} %add_convert_fusion.2.behind_ref), channel_id=1, source_target_pairs={{0,7},{1,6},{2,5},{3,4},{4,3},{5,2},{6,1},{7,0},{8,15},{9,14},{10,... | collective-permute-start | bytes 294920 | tf_op jit(solution)/shard_map/ppermute | solution.py:147
  213.6 11.3 %collective-permute-start.82 = (bf16[128,768]{1,0:T(8,128)(2,1)S(1)}, bf16[128,768]{1,0:T(8,128)(2,1)S(1)}, u32[]{:S(2)}, u32[]{:S(2)}) collective-permute-start(bf16[128,768]{1,0:T(8,128)(2,1)S(1)} %bitcast.69), channel_id=1, source_target_pairs={{0,4},{1,5},{2,6},{3,7},{4,0},{5,1},{6,2},{7,3},{8,12},{9,13},{10,... | collective-permute-start | bytes 589832 | tf_op jit(solution)/shard_map/ppermute | solution.py:147
  215.2 9.7 %collective-permute-start.83 = (bf16[128,768]{1,0:T(8,128)(2,1)S(1)}, bf16[128,768]{1,0:T(8,128)(2,1)S(1)}, u32[]{:S(2)}, u32[]{:S(2)}) collective-permute-start(bf16[128,768]{1,0:T(8,128)(2,1)S(1)} %bitcast.70), channel_id=1, source_target_pairs={{0,1},{1,0},{2,3},{3,2},{4,8},{5,9},{6,10},{7,11},{8,4},{9,5},{10,... | collective-permute-start | bytes 589832 | tf_op jit(solution)/shard_map/ppermute | solution.py:147
  (54 other events, 154.8 us)
where the time goes:
time: 227 us; the launch traced here: 226 us
  waiting for transfers between devices  112 us (49%)
  starting transfers between devices  64.7 us (29%)
  Pallas kernels  42.1 us (19%)
  other arithmetic  3.39 us (1%)
  local copies, waits for them, and re-layouts  2.47 us (1%)
    ppermute x84, waiting for transfers between devices, across(): return lax.ppermute(value, ('section', 'expert'), pairs)  112 us
    ppermute x84, starting transfers between devices, across(): return lax.ppermute(value, ('section', 'expert'), pairs)  64.7 us
    pallas_call x20, Pallas kernels, run_expert(): pl.pallas_call(functools.partial(expert_kernel, parts), out_shape=(jax.Sh...  38.3 us
  transfers between devices with their start and end apart: 84, of which 57 were waited for; matrix products, arithmetic and copies ran while one was open for 2% of the time, Pallas kernels for 4%

commit v1 on v0

--- a/solution.py
+++ b/solution.py
@@ -224,7 +224,8 @@
                 before = odd if q > 0 else not odd
                 arrived[late] = []
                 for k in range(chips):
-                    arrived[late].append(to_paired(behind, before, 2 * k + 1))
+                    flip = 2 * (chips - 1 - k) + 1
+                    arrived[late].append(to_paired(behind, before, flip))
                 arrived[q] = list(lax.optimization_barrier((behind, *arrived[q])))[1:]
             mine = sum(a.astype(jnp.float32) for a in arrived[q]).astype(jnp.bfloat16)
             if not odd:
@@ -258,8 +259,10 @@
                 masks[q], (index, nought, nought), (1,) + masks.shape[2:],
                 allow_negative_indices=False,
             )[0]
+            edge = ending or (isinstance(turn, int) and turn == 0)
+            parts = 2 if odd == (q > 0) and not edge else 1
             send, keep = run_expert(
-                2 if odd == (q > 0) else 1, mine, other, mask, gain, column, expert_in, expert_out,
+                parts, mine, other, mask, gain, column, expert_in, expert_out,
                 mine if behind is None else behind,
             )
             came = swapped(send)

time: 227 us -> 226 us (level)
  transfers between devices with their start and end apart: 84 -> 84, of which waited for: 57 -> 59; matrix products, arithmetic and copies ran while one was open for 2% -> 2% of each run, Pallas kernels for 4% -> 4%
where the time goes in v1:
time: 226 us; the launch traced here: 225 us
  waiting for transfers between devices  112 us (50%)
  starting transfers between devices  65.5 us (29%)
  Pallas kernels  41.1 us (18%)
  other arithmetic  3.39 us (2%)
  local copies, waits for them, and re-layouts  2.47 us (1%)
    ppermute x84, waiting for transfers between devices, across(): return lax.ppermute(value, ('section', 'expert'), pairs)  112 us
    ppermute x84, starting transfers between devices, across(): return lax.ppermute(value, ('section', 'expert'), pairs)  65.5 us
    pallas_call x20, Pallas kernels, run_expert(): pl.pallas_call(functools.partial(expert_kernel, parts), out_shape=(jax.Sh...  37.4 us
  transfers between devices with their start and end apart: 84, of which 59 were waited for; matrix products, arithmetic and copies ran while one was open for 2% of the time, Pallas kernels for 4%

profile of v1, /device:TPU:8, one launch (start us, length us, event | category | flops | bytes accessed | tf_op | source)
XLA Modules:
  0.0 224.9 jit_solution(9644582307018001645)
XLA Ops:
  5.4 3.8 %shard_map.64 = (bf16[768,3072]{1,0:T(8,128)(2,1)S(1)}, bf16[3072,768]{1,0:T(8,128)(2,1)S(1)}) custom-call(bf16[768,3072]{1,0:T(8,128)(2,1)} %bitcast.72, bf16[3072,768]{1,0:T(8,128)(2,1)} %bitcast.73), custom_call_target="tpu_custom_call" | custom-call | flops 4831838208 | bytes 18874368 | tf_op jit(solution)/shard_map/pallas_call | solution.py:88
  16.9 2.4 %collective-permute-start.8 = (bf16[64,768]{1,0:T(8,128)(2,1)S(1)}, bf16[64,768]{1,0:T(8,128)(2,1)S(1)}, u32[]{:S(2)}, u32[]{:S(2)}) collective-permute-start(bf16[64,768]{1,0:T(8,128)(2,1)S(1)} %add_convert_fusion.36.behind_ref), channel_id=1, source_target_pairs={{0,7},{1,6},{2,5},{3,4},{4,3},{5,2},{6,1},{7,0},{8,15},{9,14},{10,... | collective-permute-start | bytes 294920 | tf_op jit(solution)/shard_map/ppermute | solution.py:147
  19.7 2.8 %collective-permute-done.8 = bf16[64,768]{1,0:T(8,128)(2,1)S(1)} collective-permute-done((bf16[64,768]{1,0:T(8,128)(2,1)S(1)}, bf16[64,768]{1,0:T(8,128)(2,1)S(1)}, u32[]{:S(2)}, u32[]{:S(2)}) %collective-permute-start.8) | collective-permute-done | bytes 98336 | tf_op jit(solution)/shard_map/ppermute | solution.py:147
  29.7 3.9 %collective-permute-done.12 = bf16[64,768]{1,0:T(8,128)(2,1)S(1)} collective-permute-done((bf16[64,768]{1,0:T(8,128)(2,1)S(1)}, bf16[64,768]{1,0:T(8,128)(2,1)S(1)}, u32[]{:S(2)}, u32[]{:S(2)}) %collective-permute-start.12) | collective-permute-done | bytes 98336 | tf_op jit(solution)/shard_map/ppermute | solution.py:147
  36.2 2.4 %shard_map.68 = (bf16[64,768]{1,0:T(8,128)(2,1)S(1)}, bf16[64,768]{1,0:T(8,128)(2,1)S(1)}) custom-call(bf16[64,768]{1,0:T(8,128)(2,1)S(1)} %add_convert_fusion.31.mine_ref, bf16[64,768]{1,0:T(8,128)(2,1)S(1)} %collective-permute-done.14.other_ref, f32[128,128]{1,0:T(8,128)S(1)} %get-tuple-element.249.mask_ref, f32[1,768]{1,0:T(1,128)S(1)} %copy-done.1, ...), custom_call_target="tpu_custom_call" | custom-call | flops 1207959552 | bytes 9437184 | tf_op jit(solution)/shard_map/pallas_call | solution.py:105
  38.8 2.3 %collective-permute-start.16 = (bf16[64,768]{1,0:T(8,128)(2,1)S(1)}, bf16[64,768]{1,0:T(8,128)(2,1)S(1)}, u32[]{:S(2)}, u32[]{:S(2)}) collective-permute-start(bf16[64,768]{1,0:T(8,128)(2,1)S(1)} %add_convert_fusion.32.behind_ref), channel_id=1, source_target_pairs={{0,3},{1,2},{2,1},{3,0},{4,11},{5,10},{6,9},{7,8},{8,7},{9,6},{10,... | collective-permute-start | bytes 294920 | tf_op jit(solution)/shard_map/ppermute | solution.py:147
  42.5 2.7 %collective-permute-done.16 = bf16[64,768]{1,0:T(8,128)(2,1)S(1)} collective-permute-done((bf16[64,768]{1,0:T(8,128)(2,1)S(1)}, bf16[64,768]{1,0:T(8,128)(2,1)S(1)}, u32[]{:S(2)}, u32[]{:S(2)}) %collective-permute-start.16) | collective-permute-done | bytes 98336 | tf_op jit(solution)/shard_map/ppermute | solution.py:147
  48.7 2.2 shard_map.69
  54.0 3.9 %collective-permute-done.20 = bf16[64,768]{1,0:T(8,128)(2,1)S(1)} collective-permute-done((bf16[64,768]{1,0:T(8,128)(2,1)S(1)}, bf16[64,768]{1,0:T(8,128)(2,1)S(1)}, u32[]{:S(2)}, u32[]{:S(2)}) %collective-permute-start.20) | collective-permute-done | bytes 98336 | tf_op jit(solution)/shard_map/ppermute | solution.py:147
  62.3 2.4 %collective-permute-start.24 = (bf16[64,768]{1,0:T(8,128)(2,1)S(1)}, bf16[64,768]{1,0:T(8,128)(2,1)S(1)}, u32[]{:S(2)}, u32[]{:S(2)}) collective-permute-start(bf16[64,768]{1,0:T(8,128)(2,1)S(1)} %add_convert_fusion.28.behind_ref), channel_id=1, source_target_pairs={{0,7},{1,6},{2,5},{3,4},{4,3},{5,2},{6,1},{7,0},{8,15},{9,14},{10,... | collective-permute-start | bytes 294920 | tf_op jit(solution)/shard_map/ppermute | solution.py:147
  65.0 2.8 %collective-permute-done.24 = bf16[64,768]{1,0:T(8,128)(2,1)S(1)} collective-permute-done((bf16[64,768]{1,0:T(8,128)(2,1)S(1)}, bf16[64,768]{1,0:T(8,128)(2,1)S(1)}, u32[]{:S(2)}, u32[]{:S(2)}) %collective-permute-start.24) | collective-permute-done | bytes 98336 | tf_op jit(solution)/shard_map/ppermute | solution.py:147
  75.1 3.9 %collective-permute-done.28 = bf16[64,768]{1,0:T(8,128)(2,1)S(1)} collective-permute-done((bf16[64,768]{1,0:T(8,128)(2,1)S(1)}, bf16[64,768]{1,0:T(8,128)(2,1)S(1)}, u32[]{:S(2)}, u32[]{:S(2)}) %collective-permute-start.28) | collective-permute-done | bytes 98336 | tf_op jit(solution)/shard_map/ppermute | solution.py:147
  81.5 2.2 shard_map.72
  84.0 2.3 %collective-permute-start.32 = (bf16[64,768]{1,0:T(8,128)(2,1)S(1)}, bf16[64,768]{1,0:T(8,128)(2,1)S(1)}, u32[]{:S(2)}, u32[]{:S(2)}) collective-permute-start(bf16[64,768]{1,0:T(8,128)(2,1)S(1)} %add_convert_fusion.24.behind_ref), channel_id=1, source_target_pairs={{0,3},{1,2},{2,1},{3,0},{4,11},{5,10},{6,9},{7,8},{8,7},{9,6},{10,... | collective-permute-start | bytes 294920 | tf_op jit(solution)/shard_map/ppermute | solution.py:147
  87.6 2.7 %collective-permute-done.32 = bf16[64,768]{1,0:T(8,128)(2,1)S(1)} collective-permute-done((bf16[64,768]{1,0:T(8,128)(2,1)S(1)}, bf16[64,768]{1,0:T(8,128)(2,1)S(1)}, u32[]{:S(2)}, u32[]{:S(2)}) %collective-permute-start.32) | collective-permute-done | bytes 98336 | tf_op jit(solution)/shard_map/ppermute | solution.py:147
  93.9 2.4 %shard_map.73 = (bf16[64,768]{1,0:T(8,128)(2,1)S(1)}, bf16[64,768]{1,0:T(8,128)(2,1)S(1)}) custom-call(bf16[64,768]{1,0:T(8,128)(2,1)S(1)} %add_convert_fusion.21.mine_ref, bf16[64,768]{1,0:T(8,128)(2,1)S(1)} %collective-permute-done.34.other_ref, f32[128,128]{1,0:T(8,128)S(1)} %get-tuple-element.236.mask_ref, f32[1,768]{1,0:T(1,128)S(1)} %copy-done.1, ...), custom_call_target="tpu_custom_call" | custom-call | flops 1207959552 | bytes 9437184 | tf_op jit(solution)/shard_map/pallas_call | solution.py:105
  99.4 3.9 %collective-permute-done.36 = bf16[64,768]{1,0:T(8,128)(2,1)S(1)} collective-permute-done((bf16[64,768]{1,0:T(8,128)(2,1)S(1)}, bf16[64,768]{1,0:T(8,128)(2,1)S(1)}, u32[]{:S(2)}, u32[]{:S(2)}) %collective-permute-start.36) | collective-permute-done | bytes 98336 | tf_op jit(solution)/shard_map/ppermute | solution.py:147
  107.7 2.3 %collective-permute-start.40 = (bf16[64,768]{1,0:T(8,128)(2,1)S(1)}, bf16[64,768]{1,0:T(8,128)(2,1)S(1)}, u32[]{:S(2)}, u32[]{:S(2)}) collective-permute-start(bf16[64,768]{1,0:T(8,128)(2,1)S(1)} %add_convert_fusion.20.behind_ref), channel_id=1, source_target_pairs={{0,7},{1,6},{2,5},{3,4},{4,3},{5,2},{6,1},{7,0},{8,15},{9,14},{10,... | collective-permute-start | bytes 294920 | tf_op jit(solution)/shard_map/ppermute | solution.py:147
  110.4 2.8 %collective-permute-done.40 = bf16[64,768]{1,0:T(8,128)(2,1)S(1)} collective-permute-done((bf16[64,768]{1,0:T(8,128)(2,1)S(1)}, bf16[64,768]{1,0:T(8,128)(2,1)S(1)}, u32[]{:S(2)}, u32[]{:S(2)}) %collective-permute-start.40) | collective-permute-done | bytes 98336 | tf_op jit(solution)/shard_map/ppermute | solution.py:147
  120.5 3.9 %collective-permute-done.44 = bf16[64,768]{1,0:T(8,128)(2,1)S(1)} collective-permute-done((bf16[64,768]{1,0:T(8,128)(2,1)S(1)}, bf16[64,768]{1,0:T(8,128)(2,1)S(1)}, u32[]{:S(2)}, u32[]{:S(2)}) %collective-permute-start.44) | collective-permute-done | bytes 98336 | tf_op jit(solution)/shard_map/ppermute | solution.py:147
  129.4 2.2 collective-permute-start.48
  133.0 2.7 %collective-permute-done.48 = bf16[64,768]{1,0:T(8,128)(2,1)S(1)} collective-permute-done((bf16[64,768]{1,0:T(8,128)(2,1)S(1)}, bf16[64,768]{1,0:T(8,128)(2,1)S(1)}, u32[]{:S(2)}, u32[]{:S(2)}) %collective-permute-start.48) | collective-permute-done | bytes 98336 | tf_op jit(solution)/shard_map/ppermute | solution.py:147
  144.5 3.9 %collective-permute-done.52 = bf16[64,768]{1,0:T(8,128)(2,1)S(1)} collective-permute-done((bf16[64,768]{1,0:T(8,128)(2,1)S(1)}, bf16[64,768]{1,0:T(8,128)(2,1)S(1)}, u32[]{:S(2)}, u32[]{:S(2)}) %collective-permute-start.52) | collective-permute-done | bytes 98336 | tf_op jit(solution)/shard_map/ppermute | solution.py:147
  152.8 2.3 %collective-permute-start.56 = (bf16[64,768]{1,0:T(8,128)(2,1)S(1)}, bf16[64,768]{1,0:T(8,128)(2,1)S(1)}, u32[]{:S(2)}, u32[]{:S(2)}) collective-permute-start(bf16[64,768]{1,0:T(8,128)(2,1)S(1)} %add_convert_fusion.12.behind_ref), channel_id=1, source_target_pairs={{0,7},{1,6},{2,5},{3,4},{4,3},{5,2},{6,1},{7,0},{8,15},{9,14},{10,... | collective-permute-start | bytes 294920 | tf_op jit(solution)/shard_map/ppermute | solution.py:147
  155.6 2.8 %collective-permute-done.56 = bf16[64,768]{1,0:T(8,128)(2,1)S(1)} collective-permute-done((bf16[64,768]{1,0:T(8,128)(2,1)S(1)}, bf16[64,768]{1,0:T(8,128)(2,1)S(1)}, u32[]{:S(2)}, u32[]{:S(2)}) %collective-permute-start.56) | collective-permute-done | bytes 98336 | tf_op jit(solution)/shard_map/ppermute | solution.py:147
  165.6 3.9 %collective-permute-done.60 = bf16[64,768]{1,0:T(8,128)(2,1)S(1)} collective-permute-done((bf16[64,768]{1,0:T(8,128)(2,1)S(1)}, bf16[64,768]{1,0:T(8,128)(2,1)S(1)}, u32[]{:S(2)}, u32[]{:S(2)}) %collective-permute-start.60) | collective-permute-done | bytes 98336 | tf_op jit(solution)/shard_map/ppermute | solution.py:147
  172.1 2.4 %shard_map.80 = (bf16[64,768]{1,0:T(8,128)(2,1)S(1)}, bf16[64,768]{1,0:T(8,128)(2,1)S(1)}) custom-call(bf16[64,768]{1,0:T(8,128)(2,1)S(1)} %add_convert_fusion.7.mine_ref, bf16[64,768]{1,0:T(8,128)(2,1)S(1)} %collective-permute-done.62.other_ref, f32[128,128]{1,0:T(8,128)S(1)} %get-tuple-element.243.mask_ref, f32[1,768]{1,0:T(1,128)S(1)} %copy-done.1, ...), custom_call_target="tpu_custom_call" | custom-call | flops 1207959552 | bytes 9437184 | tf_op jit(solution)/shard_map/pallas_call | solution.py:105
  174.8 2.2 collective-permute-start.64
  178.4 2.7 %collective-permute-done.64 = bf16[64,768]{1,0:T(8,128)(2,1)S(1)} collective-permute-done((bf16[64,768]{1,0:T(8,128)(2,1)S(1)}, bf16[64,768]{1,0:T(8,128)(2,1)S(1)}, u32[]{:S(2)}, u32[]{:S(2)}) %collective-permute-start.64) | collective-permute-done | bytes 98336 | tf_op jit(solution)/shard_map/ppermute | solution.py:147
  190.0 3.9 %collective-permute-done.68 = bf16[64,768]{1,0:T(8,128)(2,1)S(1)} collective-permute-done((bf16[64,768]{1,0:T(8,128)(2,1)S(1)}, bf16[64,768]{1,0:T(8,128)(2,1)S(1)}, u32[]{:S(2)}, u32[]{:S(2)}) %collective-permute-start.68) | collective-permute-done | bytes 98336 | tf_op jit(solution)/shard_map/ppermute | solution.py:147
  198.3 2.3 %collective-permute-start.72 = (bf16[64,768]{1,0:T(8,128)(2,1)S(1)}, bf16[64,768]{1,0:T(8,128)(2,1)S(1)}, u32[]{:S(2)}, u32[]{:S(2)}) collective-permute-start(bf16[64,768]{1,0:T(8,128)(2,1)S(1)} %add_convert_fusion.4.behind_ref), channel_id=1, source_target_pairs={{0,7},{1,6},{2,5},{3,4},{4,3},{5,2},{6,1},{7,0},{8,15},{9,14},{10,... | collective-permute-start | bytes 294920 | tf_op jit(solution)/shard_map/ppermute | solution.py:147
  221.5 2.7 %collective-permute-done.82 = bf16[128,768]{1,0:T(8,128)(2,1)S(1)} collective-permute-done((bf16[128,768]{1,0:T(8,128)(2,1)S(1)}, bf16[128,768]{1,0:T(8,128)(2,1)S(1)}, u32[]{:S(2)}, u32[]{:S(2)}) %collective-permute-start.82) | collective-permute-done | bytes 196640 | tf_op jit(solution)/shard_map/ppermute | solution.py:147
  (228 shorter events, 132.2 us)
Async XLA Ops:
  0.8 8.4 %collective-permute-start.2 = (bf16[32,768]{1,0:T(8,128)(2,1)S(1)}, bf16[32,768]{1,0:T(8,128)(2,1)S(1)}, u32[]{:S(2)}, u32[]{:S(2)}) collective-permute-start(bf16[32,768]{1,0:T(8,128)(2,1)S(1)} %slice_bitcast_fusion.1), channel_id=1, source_target_pairs={{0,3},{1,2},{2,1},{3,0},{4,7},{5,6},{6,5},{7,4},{8,11},{9,10},{10,... | collective-permute-start | bytes 147464 | tf_op jit(solution)/shard_map/ppermute | solution.py:147
  1.8 7.5 %collective-permute-start.3 = (bf16[32,768]{1,0:T(8,128)(2,1)S(1)}, bf16[32,768]{1,0:T(8,128)(2,1)S(1)}, u32[]{:S(2)}, u32[]{:S(2)}) collective-permute-start(bf16[32,768]{1,0:T(8,128)(2,1)S(1)} %slice_bitcast_fusion.1), channel_id=1, source_target_pairs={{0,1},{1,0},{2,3},{3,2},{4,5},{5,4},{6,7},{7,6},{8,9},{9,8},{10,11... | collective-permute-start | bytes 147464 | tf_op jit(solution)/shard_map/ppermute | solution.py:147
  3.4 9.1 %collective-permute-start = (bf16[96,768]{1,0:T(8,128)(2,1)S(1)}, bf16[96,768]{1,0:T(8,128)(2,1)S(1)}, u32[]{:S(2)}, u32[]{:S(2)}) collective-permute-start(bf16[96,768]{1,0:T(8,128)(2,1)S(1)} %slice_bitcast_fusion), channel_id=1, source_target_pairs={{0,3},{1,2},{2,1},{3,0},{4,7},{5,6},{6,5},{7,4},{8,11},{9,10},{10,... | collective-permute-start | bytes 442376 | tf_op jit(solution)/shard_map/ppermute | solution.py:147
  3.6 8.9 %collective-permute-start.1 = (bf16[96,768]{1,0:T(8,128)(2,1)S(1)}, bf16[96,768]{1,0:T(8,128)(2,1)S(1)}, u32[]{:S(2)}, u32[]{:S(2)}) collective-permute-start(bf16[96,768]{1,0:T(8,128)(2,1)S(1)} %slice_bitcast_fusion), channel_id=1, source_target_pairs={{0,1},{1,0},{2,3},{3,2},{4,5},{5,4},{6,7},{7,6},{8,9},{9,8},{10,11... | collective-permute-start | bytes 442376 | tf_op jit(solution)/shard_map/ppermute | solution.py:147
  16.9 5.6 %collective-permute-start.8 = (bf16[64,768]{1,0:T(8,128)(2,1)S(1)}, bf16[64,768]{1,0:T(8,128)(2,1)S(1)}, u32[]{:S(2)}, u32[]{:S(2)}) collective-permute-start(bf16[64,768]{1,0:T(8,128)(2,1)S(1)} %add_convert_fusion.36.behind_ref), channel_id=1, source_target_pairs={{0,7},{1,6},{2,5},{3,4},{4,3},{5,2},{6,1},{7,0},{8,15},{9,14},{10,... | collective-permute-start | bytes 294920 | tf_op jit(solution)/shard_map/ppermute | solution.py:147
  28.0 5.7 %collective-permute-start.12 = (bf16[64,768]{1,0:T(8,128)(2,1)S(1)}, bf16[64,768]{1,0:T(8,128)(2,1)S(1)}, u32[]{:S(2)}, u32[]{:S(2)}) collective-permute-start(bf16[64,768]{1,0:T(8,128)(2,1)S(1)} %add_convert_fusion.34.behind_ref), channel_id=1, source_target_pairs={{0,7},{1,6},{2,5},{3,4},{4,3},{5,2},{6,1},{7,0},{8,15},{9,14},{10,... | collective-permute-start | bytes 294920 | tf_op jit(solution)/shard_map/ppermute | solution.py:147
  29.2 5.6 %collective-permute-start.13 = (bf16[64,768]{1,0:T(8,128)(2,1)S(1)}, bf16[64,768]{1,0:T(8,128)(2,1)S(1)}, u32[]{:S(2)}, u32[]{:S(2)}) collective-permute-start(bf16[64,768]{1,0:T(8,128)(2,1)S(1)} %add_convert_fusion.34.behind_ref), channel_id=1, source_target_pairs={{0,5},{1,4},{2,7},{3,6},{4,1},{5,0},{6,3},{7,2},{8,13},{9,12},{10,... | collective-permute-start | bytes 294920 | tf_op jit(solution)/shard_map/ppermute | solution.py:147
  38.8 6.4 %collective-permute-start.16 = (bf16[64,768]{1,0:T(8,128)(2,1)S(1)}, bf16[64,768]{1,0:T(8,128)(2,1)S(1)}, u32[]{:S(2)}, u32[]{:S(2)}) collective-permute-start(bf16[64,768]{1,0:T(8,128)(2,1)S(1)} %add_convert_fusion.32.behind_ref), channel_id=1, source_target_pairs={{0,3},{1,2},{2,1},{3,0},{4,11},{5,10},{6,9},{7,8},{8,7},{9,6},{10,... | collective-permute-start | bytes 294920 | tf_op jit(solution)/shard_map/ppermute | solution.py:147
  41.1 6.2 %collective-permute-start.17 = (bf16[64,768]{1,0:T(8,128)(2,1)S(1)}, bf16[64,768]{1,0:T(8,128)(2,1)S(1)}, u32[]{:S(2)}, u32[]{:S(2)}) collective-permute-start(bf16[64,768]{1,0:T(8,128)(2,1)S(1)} %add_convert_fusion.32.behind_ref), channel_id=1, source_target_pairs={{0,1},{1,0},{2,3},{3,2},{4,9},{5,8},{6,11},{7,10},{8,5},{9,4},{10,... | collective-permute-start | bytes 294920 | tf_op jit(solution)/shard_map/ppermute | solution.py:147
  51.3 6.5 %collective-permute-start.20 = (bf16[64,768]{1,0:T(8,128)(2,1)S(1)}, bf16[64,768]{1,0:T(8,128)(2,1)S(1)}, u32[]{:S(2)}, u32[]{:S(2)}) collective-permute-start(bf16[64,768]{1,0:T(8,128)(2,1)S(1)} %add_convert_fusion.30.behind_ref), channel_id=1, source_target_pairs={{0,3},{1,2},{2,1},{3,0},{4,11},{5,10},{6,9},{7,8},{8,7},{9,6},{10,... | collective-permute-start | bytes 294920 | tf_op jit(solution)/shard_map/ppermute | solution.py:147
  52.4 6.6 %collective-permute-start.21 = (bf16[64,768]{1,0:T(8,128)(2,1)S(1)}, bf16[64,768]{1,0:T(8,128)(2,1)S(1)}, u32[]{:S(2)}, u32[]{:S(2)}) collective-permute-start(bf16[64,768]{1,0:T(8,128)(2,1)S(1)} %add_convert_fusion.30.behind_ref), channel_id=1, source_target_pairs={{0,1},{1,0},{2,3},{3,2},{4,9},{5,8},{6,11},{7,10},{8,5},{9,4},{10,... | collective-permute-start | bytes 294920 | tf_op jit(solution)/shard_map/ppermute | solution.py:147
  73.3 5.6 %collective-permute-start.28 = (bf16[64,768]{1,0:T(8,128)(2,1)S(1)}, bf16[64,768]{1,0:T(8,128)(2,1)S(1)}, u32[]{:S(2)}, u32[]{:S(2)}) collective-permute-start(bf16[64,768]{1,0:T(8,128)(2,1)S(1)} %add_convert_fusion.26.behind_ref), channel_id=1, source_target_pairs={{0,7},{1,6},{2,5},{3,4},{4,3},{5,2},{6,1},{7,0},{8,15},{9,14},{10,... | collective-permute-start | bytes 294920 | tf_op jit(solution)/shard_map/ppermute | solution.py:147
  84.0 6.4 %collective-permute-start.32 = (bf16[64,768]{1,0:T(8,128)(2,1)S(1)}, bf16[64,768]{1,0:T(8,128)(2,1)S(1)}, u32[]{:S(2)}, u32[]{:S(2)}) collective-permute-start(bf16[64,768]{1,0:T(8,128)(2,1)S(1)} %add_convert_fusion.24.behind_ref), channel_id=1, source_target_pairs={{0,3},{1,2},{2,1},{3,0},{4,11},{5,10},{6,9},{7,8},{8,7},{9,6},{10,... | collective-permute-start | bytes 294920 | tf_op jit(solution)/shard_map/ppermute | solution.py:147
  86.3 6.2 %collective-permute-start.33 = (bf16[64,768]{1,0:T(8,128)(2,1)S(1)}, bf16[64,768]{1,0:T(8,128)(2,1)S(1)}, u32[]{:S(2)}, u32[]{:S(2)}) collective-permute-start(bf16[64,768]{1,0:T(8,128)(2,1)S(1)} %add_convert_fusion.24.behind_ref), channel_id=1, source_target_pairs={{0,1},{1,0},{2,3},{3,2},{4,9},{5,8},{6,11},{7,10},{8,5},{9,4},{10,... | collective-permute-start | bytes 294920 | tf_op jit(solution)/shard_map/ppermute | solution.py:147
  96.7 6.6 %collective-permute-start.36 = (bf16[64,768]{1,0:T(8,128)(2,1)S(1)}, bf16[64,768]{1,0:T(8,128)(2,1)S(1)}, u32[]{:S(2)}, u32[]{:S(2)}) collective-permute-start(bf16[64,768]{1,0:T(8,128)(2,1)S(1)} %add_convert_fusion.22.behind_ref), channel_id=1, source_target_pairs={{0,3},{1,2},{2,1},{3,0},{4,11},{5,10},{6,9},{7,8},{8,7},{9,6},{10,... | collective-permute-start | bytes 294920 | tf_op jit(solution)/shard_map/ppermute | solution.py:147
  97.8 6.6 %collective-permute-start.37 = (bf16[64,768]{1,0:T(8,128)(2,1)S(1)}, bf16[64,768]{1,0:T(8,128)(2,1)S(1)}, u32[]{:S(2)}, u32[]{:S(2)}) collective-permute-start(bf16[64,768]{1,0:T(8,128)(2,1)S(1)} %add_convert_fusion.22.behind_ref), channel_id=1, source_target_pairs={{0,1},{1,0},{2,3},{3,2},{4,9},{5,8},{6,11},{7,10},{8,5},{9,4},{10,... | collective-permute-start | bytes 294920 | tf_op jit(solution)/shard_map/ppermute | solution.py:147
  118.7 5.7 %collective-permute-start.44 = (bf16[64,768]{1,0:T(8,128)(2,1)S(1)}, bf16[64,768]{1,0:T(8,128)(2,1)S(1)}, u32[]{:S(2)}, u32[]{:S(2)}) collective-permute-start(bf16[64,768]{1,0:T(8,128)(2,1)S(1)} %add_convert_fusion.18.behind_ref), channel_id=1, source_target_pairs={{0,7},{1,6},{2,5},{3,4},{4,3},{5,2},{6,1},{7,0},{8,15},{9,14},{10,... | collective-permute-start | bytes 294920 | tf_op jit(solution)/shard_map/ppermute | solution.py:147
  119.9 5.6 %collective-permute-start.45 = (bf16[64,768]{1,0:T(8,128)(2,1)S(1)}, bf16[64,768]{1,0:T(8,128)(2,1)S(1)}, u32[]{:S(2)}, u32[]{:S(2)}) collective-permute-start(bf16[64,768]{1,0:T(8,128)(2,1)S(1)} %add_convert_fusion.18.behind_ref), channel_id=1, source_target_pairs={{0,5},{1,4},{2,7},{3,6},{4,1},{5,0},{6,3},{7,2},{8,13},{9,12},{10,... | collective-permute-start | bytes 294920 | tf_op jit(solution)/shard_map/ppermute | solution.py:147
  129.4 6.4 %collective-permute-start.48 = (bf16[64,768]{1,0:T(8,128)(2,1)S(1)}, bf16[64,768]{1,0:T(8,128)(2,1)S(1)}, u32[]{:S(2)}, u32[]{:S(2)}) collective-permute-start(bf16[64,768]{1,0:T(8,128)(2,1)S(1)} %add_convert_fusion.16.behind_ref), channel_id=1, source_target_pairs={{0,3},{1,2},{2,1},{3,0},{4,11},{5,10},{6,9},{7,8},{8,7},{9,6},{10,... | collective-permute-start | bytes 294920 | tf_op jit(solution)/shard_map/ppermute | solution.py:147
  131.6 6.3 %collective-permute-start.49 = (bf16[64,768]{1,0:T(8,128)(2,1)S(1)}, bf16[64,768]{1,0:T(8,128)(2,1)S(1)}, u32[]{:S(2)}, u32[]{:S(2)}) collective-permute-start(bf16[64,768]{1,0:T(8,128)(2,1)S(1)} %add_convert_fusion.16.behind_ref), channel_id=1, source_target_pairs={{0,1},{1,0},{2,3},{3,2},{4,9},{5,8},{6,11},{7,10},{8,5},{9,4},{10,... | collective-permute-start | bytes 294920 | tf_op jit(solution)/shard_map/ppermute | solution.py:147
  141.9 6.6 %collective-permute-start.52 = (bf16[64,768]{1,0:T(8,128)(2,1)S(1)}, bf16[64,768]{1,0:T(8,128)(2,1)S(1)}, u32[]{:S(2)}, u32[]{:S(2)}) collective-permute-start(bf16[64,768]{1,0:T(8,128)(2,1)S(1)} %add_convert_fusion.14.behind_ref), channel_id=1, source_target_pairs={{0,3},{1,2},{2,1},{3,0},{4,11},{5,10},{6,9},{7,8},{8,7},{9,6},{10,... | collective-permute-start | bytes 294920 | tf_op jit(solution)/shard_map/ppermute | solution.py:147
  143.0 6.6 %collective-permute-start.53 = (bf16[64,768]{1,0:T(8,128)(2,1)S(1)}, bf16[64,768]{1,0:T(8,128)(2,1)S(1)}, u32[]{:S(2)}, u32[]{:S(2)}) collective-permute-start(bf16[64,768]{1,0:T(8,128)(2,1)S(1)} %add_convert_fusion.14.behind_ref), channel_id=1, source_target_pairs={{0,1},{1,0},{2,3},{3,2},{4,9},{5,8},{6,11},{7,10},{8,5},{9,4},{10,... | collective-permute-start | bytes 294920 | tf_op jit(solution)/shard_map/ppermute | solution.py:147
  163.9 5.7 %collective-permute-start.60 = (bf16[64,768]{1,0:T(8,128)(2,1)S(1)}, bf16[64,768]{1,0:T(8,128)(2,1)S(1)}, u32[]{:S(2)}, u32[]{:S(2)}) collective-permute-start(bf16[64,768]{1,0:T(8,128)(2,1)S(1)} %add_convert_fusion.10.behind_ref), channel_id=1, source_target_pairs={{0,7},{1,6},{2,5},{3,4},{4,3},{5,2},{6,1},{7,0},{8,15},{9,14},{10,... | collective-permute-start | bytes 294920 | tf_op jit(solution)/shard_map/ppermute | solution.py:147
  165.1 5.6 %collective-permute-start.61 = (bf16[64,768]{1,0:T(8,128)(2,1)S(1)}, bf16[64,768]{1,0:T(8,128)(2,1)S(1)}, u32[]{:S(2)}, u32[]{:S(2)}) collective-permute-start(bf16[64,768]{1,0:T(8,128)(2,1)S(1)} %add_convert_fusion.10.behind_ref), channel_id=1, source_target_pairs={{0,5},{1,4},{2,7},{3,6},{4,1},{5,0},{6,3},{7,2},{8,13},{9,12},{10,... | collective-permute-start | bytes 294920 | tf_op jit(solution)/shard_map/ppermute | solution.py:147
  174.8 6.4 %collective-permute-start.64 = (bf16[64,768]{1,0:T(8,128)(2,1)S(1)}, bf16[64,768]{1,0:T(8,128)(2,1)S(1)}, u32[]{:S(2)}, u32[]{:S(2)}) collective-permute-start(bf16[64,768]{1,0:T(8,128)(2,1)S(1)} %add_convert_fusion.8.behind_ref), channel_id=1, source_target_pairs={{0,3},{1,2},{2,1},{3,0},{4,11},{5,10},{6,9},{7,8},{8,7},{9,6},{10,... | collective-permute-start | bytes 294920 | tf_op jit(solution)/shard_map/ppermute | solution.py:147
  177.0 6.3 %collective-permute-start.65 = (bf16[64,768]{1,0:T(8,128)(2,1)S(1)}, bf16[64,768]{1,0:T(8,128)(2,1)S(1)}, u32[]{:S(2)}, u32[]{:S(2)}) collective-permute-start(bf16[64,768]{1,0:T(8,128)(2,1)S(1)} %add_convert_fusion.8.behind_ref), channel_id=1, source_target_pairs={{0,1},{1,0},{2,3},{3,2},{4,9},{5,8},{6,11},{7,10},{8,5},{9,4},{10,... | collective-permute-start | bytes 294920 | tf_op jit(solution)/shard_map/ppermute | solution.py:147
  187.3 6.6 %collective-permute-start.68 = (bf16[64,768]{1,0:T(8,128)(2,1)S(1)}, bf16[64,768]{1,0:T(8,128)(2,1)S(1)}, u32[]{:S(2)}, u32[]{:S(2)}) collective-permute-start(bf16[64,768]{1,0:T(8,128)(2,1)S(1)} %add_convert_fusion.6.behind_ref), channel_id=1, source_target_pairs={{0,3},{1,2},{2,1},{3,0},{4,11},{5,10},{6,9},{7,8},{8,7},{9,6},{10,... | collective-permute-start | bytes 294920 | tf_op jit(solution)/shard_map/ppermute | solution.py:147
  188.4 6.6 %collective-permute-start.69 = (bf16[64,768]{1,0:T(8,128)(2,1)S(1)}, bf16[64,768]{1,0:T(8,128)(2,1)S(1)}, u32[]{:S(2)}, u32[]{:S(2)}) collective-permute-start(bf16[64,768]{1,0:T(8,128)(2,1)S(1)} %add_convert_fusion.6.behind_ref), channel_id=1, source_target_pairs={{0,1},{1,0},{2,3},{3,2},{4,9},{5,8},{6,11},{7,10},{8,5},{9,4},{10,... | collective-permute-start | bytes 294920 | tf_op jit(solution)/shard_map/ppermute | solution.py:147
  201.0 7.0 %collective-permute-start.77 = (bf16[64,768]{1,0:T(8,128)(2,1)S(1)}, bf16[64,768]{1,0:T(8,128)(2,1)S(1)}, u32[]{:S(2)}, u32[]{:S(2)}) collective-permute-start(bf16[64,768]{1,0:T(8,128)(2,1)S(1)} %add_convert_fusion.2.behind_ref), channel_id=1, source_target_pairs={{0,7},{1,6},{2,5},{3,4},{4,3},{5,2},{6,1},{7,0},{8,15},{9,14},{10,... | collective-permute-start | bytes 294920 | tf_op jit(solution)/shard_map/ppermute | solution.py:147
  202.4 7.7 %collective-permute-start.78 = (bf16[64,768]{1,0:T(8,128)(2,1)S(1)}, bf16[64,768]{1,0:T(8,128)(2,1)S(1)}, u32[]{:S(2)}, u32[]{:S(2)}) collective-permute-start(bf16[64,768]{1,0:T(8,128)(2,1)S(1)} %add_convert_fusion.2.behind_ref), channel_id=1, source_target_pairs={{0,5},{1,4},{2,7},{3,6},{4,1},{5,0},{6,3},{7,2},{8,13},{9,12},{10,... | collective-permute-start | bytes 294920 | tf_op jit(solution)/shard_map/ppermute | solution.py:147
  212.7 11.4 %collective-permute-start.82 = (bf16[128,768]{1,0:T(8,128)(2,1)S(1)}, bf16[128,768]{1,0:T(8,128)(2,1)S(1)}, u32[]{:S(2)}, u32[]{:S(2)}) collective-permute-start(bf16[128,768]{1,0:T(8,128)(2,1)S(1)} %bitcast.69), channel_id=1, source_target_pairs={{0,4},{1,5},{2,6},{3,7},{4,0},{5,1},{6,2},{7,3},{8,12},{9,13},{10,... | collective-permute-start | bytes 589832 | tf_op jit(solution)/shard_map/ppermute | solution.py:147
  214.2 9.9 %collective-permute-start.83 = (bf16[128,768]{1,0:T(8,128)(2,1)S(1)}, bf16[128,768]{1,0:T(8,128)(2,1)S(1)}, u32[]{:S(2)}, u32[]{:S(2)}) collective-permute-start(bf16[128,768]{1,0:T(8,128)(2,1)S(1)} %bitcast.70), channel_id=1, source_target_pairs={{0,1},{1,0},{2,3},{3,2},{4,8},{5,9},{6,10},{7,11},{8,4},{9,5},{10,... | collective-permute-start | bytes 589832 | tf_op jit(solution)/shard_map/ppermute | solution.py:147
  (54 other events, 161.5 us)
